TPU v7x, 32 devices: a whole 2x2x4 slice. The times are simulated.
32 devices in a mesh: shift: 8 (over y, x, core), dom: 4 (over z).
Axes of the slice: x: 2, y: 2, z: 4, core: 2. Of those that a mesh axis runs over, the one named last changes fastest.
Arguments:
- samples: float32 [32, 64, 1024], P('dom'), may hold values from -6 to 6
- potential: float32 [32, 1024], P('dom'), may hold values from 0 to 4
Outputs:
- subspace: float32 [32, 64, 1024], P('dom')
- reduced_h: float32 [64, 64], replicated
- reduced_b: float32 [64, 64], replicated
All inputs are finite; a program needn't handle non-finite values.
Results may differ from a plain program's by a relative error of at most 0.00027.
Values sent between devices are 32-bit elements; how exact they have to be, the bound alone decides.
No kernel may reach another device: no remote copies, remote signals or barrier semaphores. Data moves between devices by JAX's collectives and lax.ppermute only.
A program may use at most 128 MiB of HBM per device.

v0:
```python
import jax
import jax.numpy as jnp
from jax import lax
from jax.sharding import PartitionSpec as P

NX = 32
NY = 32
CENTRE = 3.0
RADIUS = 2.0
RIDGE = 0.01


def extended_2(x, sides, width):
    for axis, dim in sides:
        count, length = (lax.axis_size(axis), x.shape[dim])
        up = [(i, (i + 1) % count) for i in range(count - 1)]
        down = [(j, i) for i, j in up]
        last = lax.slice_in_dim(x, length - width, length, axis=dim)
        first = lax.slice_in_dim(x, 0, width, axis=dim)
        before = lax.ppermute(last, axis, up)
        after = lax.ppermute(first, axis, down)
        x = jnp.concatenate([before, x, after], axis=dim)
    return x


def plane_sum(values):
    extent = values.shape[-1]
    leading = [(0, 0)] * (values.ndim - 1)
    padded = jnp.pad(values, leading + [(NY, NY)])
    column = lax.broadcasted_iota(jnp.int32, (extent,), 0) % NY
    lower_ok = (column != 0).astype(values.dtype)
    upper_ok = (column != NY - 1).astype(values.dtype)
    return (
        padded[..., 0:extent]
        + padded[..., 2 * NY : 2 * NY + extent]
        + padded[..., NY - 1 : NY - 1 + extent] * lower_ok
        + padded[..., NY + 1 : NY + 1 + extent] * upper_ok
    )


def colsum(values):
    return jnp.sum(values, axis=(0, 2))


def on_device(samples, potential):
    nodes = lax.axis_size("shift")
    planes = samples.shape[0]
    order = lax.axis_index("shift").astype(jnp.float32)
    angle = jnp.pi * (order + 0.5) / nodes
    shift_re = CENTRE + RADIUS * jnp.cos(angle)
    shift_im = RADIUS * jnp.sin(angle)
    weight_re = RADIUS * jnp.cos(angle) / nodes
    weight_im = RADIUS * jnp.sin(angle) / nodes

    def inverses(onsite_part):
        diag_re = shift_re - onsite_part
        modulus = diag_re * diag_re + shift_im * shift_im
        return (diag_re / modulus, -shift_im / modulus)

    def apply_inv(vector, inv_pair):
        return jnp.stack(
            [
                vector[0] * inv_pair[0] - vector[1] * inv_pair[1],
                vector[0] * inv_pair[1] + vector[1] * inv_pair[0],
            ]
        )

    def combine(vector, hamil):
        return jnp.stack(
            [
                shift_re * vector[0] - shift_im * vector[1] - hamil[0],
                shift_re * vector[1] + shift_im * vector[0] - hamil[1],
            ]
        )

    onsite = (6.0 + potential)[:, None, :]
    inv_own = inverses(onsite)

    def shrink_operate(vector, onsite_inner):
        inner = vector[:, 1:-1]
        beside = vector[:, 2:] + vector[:, :-2] + plane_sum(inner)
        return combine(inner, onsite_inner * inner - beside)

    joined = jnp.concatenate([samples, potential[:, None, :]], axis=1)
    extended = extended_2(joined, (("dom", 0),), 2)
    ext_samples = extended[:, :-1]
    ext_onsite = 6.0 + extended[:, -1:]
    inv_ext = inverses(ext_onsite)
    first_ext = apply_inv(jnp.stack([ext_samples, jnp.zeros_like(ext_samples)]), inv_ext)
    image_ext = shrink_operate(first_ext, ext_onsite[1:-1])
    total_planes = planes * lax.axis_size("dom")
    plane_index = (
        lax.axis_index("dom") * planes - 1 + lax.broadcasted_iota(jnp.int32, (planes + 2,), 0)
    )
    inside = ((plane_index >= 0) & (plane_index < total_planes)).astype(jnp.float32)
    image_ext = image_ext * inside[None, :, None, None]
    image_one = image_ext[:, 1:-1]
    first_block_real = image_one[0]
    first_block_imag = image_one[1]
    first_set = jnp.stack(
        [
            colsum(first_block_real * first_block_real + first_block_imag * first_block_imag),
            colsum(first_block_real * samples),
            colsum(-first_block_imag * samples),
        ]
    )
    first_tot = lax.psum(first_set, "dom")
    inv_mid = (inv_ext[0][1:-1], inv_ext[1][1:-1])
    image_two = shrink_operate(apply_inv(image_ext, inv_mid), ext_onsite[2:-2])
    two_re = image_two[0]
    two_im = image_two[1]
    second_set = jnp.stack(
        [
            colsum(first_block_real * two_re + first_block_imag * two_im),
            colsum(first_block_real * two_im - first_block_imag * two_re),
            colsum(two_re * two_re + two_im * two_im),
            colsum(two_re * samples),
            colsum(-two_im * samples),
        ]
    )
    second_tot = lax.psum(second_set, "dom")
    totals = jnp.concatenate([first_tot, second_tot], axis=0)
    g_one = totals[0]
    q_one_re = totals[1]
    q_one_im = totals[2]
    g_mix_re = totals[3]
    g_mix_im = totals[4]
    g_two = totals[5]
    q_two_re = totals[6]
    q_two_im = totals[7]
    ridge = RIDGE * (g_one + g_two) / 2.0
    determ = (g_one + ridge) * (g_two + ridge) - (g_mix_re * g_mix_re + g_mix_im * g_mix_im)
    coef_one_re = (
        (g_two + ridge) * q_one_re - (g_mix_re * q_two_re - g_mix_im * q_two_im)
    ) / determ
    coef_one_im = (
        (g_two + ridge) * q_one_im - (g_mix_re * q_two_im + g_mix_im * q_two_re)
    ) / determ
    coef_two_re = (
        (g_one + ridge) * q_two_re - (g_mix_re * q_one_re + g_mix_im * q_one_im)
    ) / determ
    coefficient_second_imag = (
        (g_one + ridge) * q_two_im - (g_mix_re * q_one_im - g_mix_im * q_one_re)
    ) / determ
    first_coefficient_real = coef_one_re[None, :, None]
    first_coefficient_imag = coef_one_im[None, :, None]
    second_coefficient_real = coef_two_re[None, :, None]
    second_coefficient_imag = coefficient_second_imag[None, :, None]
    solution = apply_inv(
        jnp.stack(
            [
                first_coefficient_real * samples
                + second_coefficient_real * first_block_real
                - second_coefficient_imag * first_block_imag,
                first_coefficient_imag * samples
                + second_coefficient_real * first_block_imag
                + second_coefficient_imag * first_block_real,
            ]
        ),
        inv_own,
    )
    weighted = weight_re * solution[0] - weight_im * solution[1]
    scale = 1.0 / (NX * NY * planes * lax.axis_size("dom"))
    subspace = lax.psum(weighted, "shift")
    padded = extended_2(subspace, (("dom", 0),), 1)
    applied = onsite * subspace - (padded[2:] + padded[:-2] + plane_sum(subspace))
    part_h = jnp.einsum("znc,zmc->nm", subspace, applied, precision=lax.Precision.HIGHEST) * scale
    part_b = jnp.einsum("znc,zmc->nm", subspace, subspace, precision=lax.Precision.HIGHEST) * scale
    reduced_h, reduced_b = lax.psum((part_h, part_b), "dom")
    return (subspace, reduced_h, reduced_b)


def solution(mesh):
    in_specs = (P("dom", None, None), P("dom", None))
    out_specs = (P("dom", None, None), P(), P())
    return jax.shard_map(
        on_device, mesh=mesh, in_specs=in_specs, out_specs=out_specs, check_vma=False
    )
```

profile of v0, /device:TPU:0, one launch (start us, length us, event | category | flops | bytes accessed | tf_op | source)
XLA Modules:
  0.0 185.9 jit_solution(1204473247824905076)
XLA Ops:
  7.2 1.7 constant_dynamic-update-slice_fusion
  9.7 5.0 %collective-permute-start = (f32[2,65,1024]{2,0,1:T(2,128)S(1)}, f32[2,65,1024]{2,0,1:T(2,128)S(1)}, u32[]{:S(2)}, u32[]{:S(2)}) collective-permute-start(f32[2,65,1024]{2,0,1:T(2,128)S(1)} %copy.8), channel_id=1, source_target_pairs={{0,1},{1,2},{2,3},{4,5},{5,6},{6,7},{8,9},{9,10},{10,11},{12,13},{... | collective-permute-start | bytes 1597448 | tf_op jit(solution)/shard_map/ppermute | solution.py:20
  14.7 1.2 copy.9
  15.9 1.3 collective-permute-start.1
  18.0 8.0 %collective-permute-done = f32[2,65,1024]{2,0,1:T(2,128)S(1)} collective-permute-done((f32[2,65,1024]{2,0,1:T(2,128)S(1)}, f32[2,65,1024]{2,0,1:T(2,128)S(1)}, u32[]{:S(2)}, u32[]{:S(2)}) %collective-permute-start) | collective-permute-done | bytes 532512 | tf_op jit(solution)/shard_map/ppermute | solution.py:20
  26.1 5.5 %collective-permute-done.1 = f32[2,65,1024]{2,0,1:T(2,128)} collective-permute-done((f32[2,65,1024]{2,0,1:T(2,128)}, f32[2,65,1024]{2,0,1:T(2,128)}, u32[]{:S(2)}, u32[]{:S(2)}) %collective-permute-start.1) | collective-permute-done | bytes 532512 | tf_op jit(solution)/shard_map/ppermute | solution.py:21
  31.6 1.2 copy.11
  34.6 2.8 %fusion.9 = f32[2,10,64,1024]{3,2,1,0:T(8,128)} fusion(f32[1,12,64,1024]{3,2,1,0:T(8,128)S(1)} %get-tuple-element.29, f32[1,12,64,1024]{3,2,1,0:T(8,128)S(1)} %get-tuple-element.28), kind=kLoop, calls=%fused_computation.21 | loop fusion | flops 1310720 | bytes 11534336 | tf_op jit(solution)/shard_map/stack | solution.py:61
  37.4 13.4 %fusion.4 = f32[2,10,64,1024]{3,2,1,0:T(8,128)} fusion(f32[2,10,64,1024]{3,2,1,0:T(8,128)} %fusion.9, f32[1,12,64,1024]{3,2,1,0:T(8,128)S(1)} %get-tuple-element.29, f32[1,12,64,1024]{3,2,1,0:T(8,128)S(1)} %get-tuple-element.28, f32[1024]{0:T(1024)S(1)} %get-tuple-element.45, f32[1024]{0:T(1024)S(1)} %get-tuple-element.44, f32[10,1024]{1,0:T(8,128)S(1)} %bitcast.188), kind=kLoop, calls=%fused_computation.16 | loop fusion | flops 14417920 | bytes 16826368 | tf_op jit(solution)/shard_map/sub | solution.py:82
  50.8 3.8 %slice_subtract_fusion.1 = (f32[1,10,64,1024]{3,2,1,0:T(8,128)S(1)}, f32[1,10,64,1024]{3,2,1,0:T(8,128)S(1)}) fusion(f32[2,10,64,1024]{3,2,1,0:T(8,128)} %fusion.4, f32[1,12,64,1024]{3,2,1,0:T(8,128)S(1)} %get-tuple-element.28, f32[1,12,64,1024]{3,2,1,0:T(8,128)S(1)} %get-tuple-element.29, f32[]{:T(128)S(6)} %mul.491, f32[]{:T(128)S(6)} %add_shard_map.3), kind=kLoop, calls=%fused_computation.43 | loop fusion | flops 5242880 | bytes 15728648 | tf_op jit(solution)/shard_map/sub | solution.py:71
  55.6 1.3 multiply_add_fusion
  57.4 4.8 %fusion.14 = f32[2,8,64,1024]{3,2,1,0:T(8,128)S(1)} fusion(f32[2,8,64,1024]{3,2,1,0:T(8,128)S(1)} %fusion.19, f32[1,10,64,1024]{3,2,1,0:T(8,128)S(1)} %get-tuple-element.27, f32[1,10,64,1024]{3,2,1,0:T(8,128)S(1)} %get-tuple-element.26, f32[1024]{0:T(1024)S(1)} %get-tuple-element.45, f32[1024]{0:T(1024)S(1)} %get-tuple-element.44, f32[8,1024]{1,0:T(8,128)S(1)} %bitcast.189), kind=kLoop, calls=%fused_computation.32 | loop fusion | flops 11534336 | bytes 13672448 | tf_op jit(solution)/shard_map/sub | solution.py:82
  62.3 1.5 fusion.36
  63.9 2.0 %multiply_reduce_fusion.1 = (f32[64]{0:T(128)S(1)}, f32[64]{0:T(128)S(1)}, f32[64]{0:T(128)S(1)}, f32[64]{0:T(128)S(1)}, f32[64]{0:T(128)S(1)}, /*index=5*/f32[64]{0:T(128)S(1)}, f32[64]{0:T(128)S(1)}, f32[64]{0:T(128)S(1)}) fusion(f32[8,64,1024]{2,1,0:T(8,128)S(1)} %copy-done.2, f32[2,10,64,1024]{3,2,1,0:T(8,128)S(1)} %maximum_multiply_fusion, ...), kind=kLoop, calls=%fused_computation.72 | loop fusion | flops 13630976 | bytes 10487808 | tf_op jit(solution)/shard_map/reduce_sum | solution.py:42
  66.0 10.3 %all-reduce.4 = (f32[5,64]{1,0:T(8,128)S(1)}, f32[3,64]{1,0:T(4,128)S(1)}) all-reduce(f32[5,64]{1,0:T(8,128)S(1)} %stack.59, f32[3,64]{1,0:T(4,128)S(1)} %pad_maximum_fusion.6), channel_id=1, replica_groups=mesh['shift'=8,'dom'=4] {'dom'}, use_global_device_ids=true, to_apply=%region_5.6 | all-reduce | flops 512 | bytes 4096 | tf_op jit(solution)/shard_map/psum | solution.py:121
  76.3 4.9 %multiply_subtract_fusion.1 = f32[8,64,1024]{2,1,0:T(8,128)} fusion(f32[8,64,1024]{2,1,0:T(8,128)S(1)} %copy-done.2, f32[2,10,64,1024]{3,2,1,0:T(8,128)} %copy-done, f32[]{:T(128)S(6)} %div.77, f32[8,1024]{1,0:T(8,128)S(1)} %get-tuple-element.38, f32[64]{0:T(128)S(1)} %fusion.65, f32[8,1024]{1,0:T(8,128)S(1)} %get-tuple-element.39, ...), kind=kLoop, calls=%fused_computation.70 | loop fusion | flops 9961472 | bytes 8455176 | tf_op jit(solution)/shard_map/sub | solution.py:162
  81.3 60.2 %all-reduce.7.cloned.1.call-done = f32[8,64,1024]{2,1,0:T(8,128)} async-done(((f32[8,64,1024]{2,1,0:T(8,128)}), f32[8,64,1024]{2,1,0:T(8,128)}) %all-reduce.7.cloned.1.call-update) | async-done | bytes 2097168 | tf_op jit(solution)/shard_map/psum | solution.py:164
  141.5 1.2 fusion.78
  142.7 1.3 collective-permute-start.2
  144.0 4.6 %collective-permute-start.3 = (f32[1,64,1024]{2,1,0:T(8,128)S(1)}, f32[1,64,1024]{2,1,0:T(8,128)S(1)}, u32[]{:S(2)}, u32[]{:S(2)}) collective-permute-start(f32[1,64,1024]{2,1,0:T(8,128)S(1)} %get-tuple-element.33), channel_id=1, source_target_pairs={{0,1},{1,2},{2,3},{4,5},{5,6},{6,7},{8,9},{9,10},{10,11},{12,13},{... | collective-permute-start | bytes 786440 | tf_op jit(solution)/shard_map/ppermute | solution.py:20
  148.6 4.0 %fusion.41 = f32[64,64]{1,0:T(8,128)S(1)} fusion(f32[8,64,1024]{2,1,0:T(8,128)} %all-reduce.7.cloned.1.call-done), kind=kOutput, calls=%fused_computation.81 | convolution fusion | flops 402657280 | bytes 2113536 | tf_op jit(solution)/shard_map/znc,zmc->nm/dot_general | solution.py:168
  152.7 3.8 %fusion.42 = f32[64,64]{1,0:T(8,128)S(1)} fusion(f32[8,64,1024]{2,1,0:T(8,128)S(1)} %copy-done.1, f32[1,64,1024]{2,1,0:T(8,128)S(1)} %collective-permute-done.3, f32[1,64,1024]{2,1,0:T(8,128)S(1)} %collective-permute-done.2, f32[1024]{0:T(1024)S(1)} %get-tuple-element.45, f32[1024]{0:T(1024)S(1)} %get-tuple-element.44, f32[8,1024]{1,0:T(8,128)S(1)} %copy-done.5), kind=kOutput, calls=%fused_computation.82 | convolution fusion | flops 408424448 | bytes 4775936 | tf_op jit(solution)/shard_map/znc,zmc->nm/dot_general | solution.py:167
  156.5 21.2 %all-reduce.3 = (f32[64,64]{1,0:T(8,128)}, f32[64,64]{1,0:T(8,128)}) all-reduce(f32[64,64]{1,0:T(8,128)S(1)} %fusion.42, f32[64,64]{1,0:T(8,128)S(1)} %fusion.41), channel_id=1, replica_groups=mesh['shift'=8,'dom'=4] {'dom'}, use_global_device_ids=true, to_apply=%region_11.12 | all-reduce | flops 8192 | bytes 65536 | tf_op jit(solution)/shard_map/psum | solution.py:169
  177.7 1.3 copy.40
  (45 shorter events, 5.0 us)
Async XLA Ops:
  7.2 1.8 copy-start.4
  7.2 134.3 %all-reduce.7.cloned.1.call-start = ((), (), s32[]{:S(2)}) async-start(), calls=%async_computation | async-start | bytes 4194304 | tf_op jit(solution)/shard_map/psum | solution.py:164
  9.7 16.3 %collective-permute-start = (f32[2,65,1024]{2,0,1:T(2,128)S(1)}, f32[2,65,1024]{2,0,1:T(2,128)S(1)}, u32[]{:S(2)}, u32[]{:S(2)}) collective-permute-start(f32[2,65,1024]{2,0,1:T(2,128)S(1)} %copy.8), channel_id=1, source_target_pairs={{0,1},{1,2},{2,3},{4,5},{5,6},{6,7},{8,9},{9,10},{10,11},{12,13},{... | collective-permute-start | bytes 1597448 | tf_op jit(solution)/shard_map/ppermute | solution.py:20
  15.9 15.8 %collective-permute-start.1 = (f32[2,65,1024]{2,0,1:T(2,128)}, f32[2,65,1024]{2,0,1:T(2,128)}, u32[]{:S(2)}, u32[]{:S(2)}) collective-permute-start(f32[2,65,1024]{2,0,1:T(2,128)} %copy.9), channel_id=1, source_target_pairs={{1,0},{2,1},{3,2},{5,4},{6,5},{7,6},{9,8},{10,9},{11,10},{13,12},{... | collective-permute-start | bytes 1597448 | tf_op jit(solution)/shard_map/ppermute | solution.py:21
  33.0 0.7 copy-start.3
  50.8 3.9 %slice-start = ((f32[12,1,1024]{2,1,0:T(1,128)}), f32[10,1,1024]{2,1,0:T(1,128)S(1)}, s32[]{:S(2)}) async-start(f32[12,1,1024]{2,1,0:T(1,128)} %copy-done.3), calls=%async_computation.1 | async-start | bytes 81920 | tf_op jit(solution)/shard_map/slice | solution.py:108
  55.6 8.2 %copy-start = (f32[2,10,64,1024]{3,2,1,0:T(8,128)}, f32[2,10,64,1024]{3,2,1,0:T(8,128)S(1)}, u32[]{:S(2)}) copy-start(f32[2,10,64,1024]{3,2,1,0:T(8,128)S(1)} %maximum_multiply_fusion) | copy-start | bytes 15728644
  62.3 1.6 copy-start.2
  81.2 71.4 %copy-start.5 = (f32[8,1024]{1,0:T(8,128)S(1)}, f32[8,1024]{1,0:T(8,128)}, u32[]{:S(2)}) copy-start(f32[8,1024]{1,0:T(8,128)} %get-tuple-element.37) | copy-start | bytes 98308
  141.5 11.2 %copy-start.1 = (f32[8,64,1024]{2,1,0:T(8,128)S(1)}, f32[8,64,1024]{2,1,0:T(8,128)}, u32[]{:S(2)}) copy-start(f32[8,64,1024]{2,1,0:T(8,128)} %all-reduce.7.cloned.1.call-done) | copy-start | bytes 6291460
  142.7 9.9 %collective-permute-start.2 = (f32[1,64,1024]{2,1,0:T(8,128)S(1)}, f32[1,64,1024]{2,1,0:T(8,128)S(1)}, u32[]{:S(2)}, u32[]{:S(2)}) collective-permute-start(f32[1,64,1024]{2,1,0:T(8,128)S(1)} %get-tuple-element.32), channel_id=1, source_target_pairs={{1,0},{2,1},{3,2},{5,4},{6,5},{7,6},{9,8},{10,9},{11,10},{13,12},{... | collective-permute-start | bytes 786440 | tf_op jit(solution)/shard_map/ppermute | solution.py:21
  144.0 8.7 %collective-permute-start.3 = (f32[1,64,1024]{2,1,0:T(8,128)S(1)}, f32[1,64,1024]{2,1,0:T(8,128)S(1)}, u32[]{:S(2)}, u32[]{:S(2)}) collective-permute-start(f32[1,64,1024]{2,1,0:T(8,128)S(1)} %get-tuple-element.33), channel_id=1, source_target_pairs={{0,1},{1,2},{2,3},{4,5},{5,6},{6,7},{8,9},{9,10},{10,11},{12,13},{... | collective-permute-start | bytes 786440 | tf_op jit(solution)/shard_map/ppermute | solution.py:20
Sparse Core Ops, SparseCore 0:
  81.4 60.0 all-reduce.6
where the time goes:
time: 186 us
  waiting for transfers between devices  73.8 us (40%)
  other arithmetic  38.1 us (20%)
  blocking collectives  31.5 us (17%)
  between operations  14.5 us (8%)
  starting transfers between devices  12.2 us (7%)
  local copies, waits for them, and re-layouts  7.97 us (4%)
  matrix products  7.85 us (4%)
    psum x1, waiting for transfers between devices, on_device(): subspace = lax.psum(weighted, 'shift')  60.2 us
    psum x1, blocking collectives, on_device(): reduced_h, reduced_b = lax.psum((part_h, part_b), 'dom')  21.2 us
    sub x2, other arithmetic, shrink_operate(): return combine(inner, onsite_inner * inner - beside)  18.2 us
    psum x1, blocking collectives, on_device(): second_tot = lax.psum(second_set, 'dom')  10.3 us
    ppermute x2, starting transfers between devices, extended_2(): before = lax.ppermute(last, axis, up)  9.55 us
    ppermute x2, waiting for transfers between devices, extended_2(): before = lax.ppermute(last, axis, up)  8.03 us
    ppermute x2, waiting for transfers between devices, extended_2(): after = lax.ppermute(first, axis, down)  5.49 us
    sub x2, other arithmetic, combine(): shift_re * vector[0] - shift_im * vector[1] - hamil[0]  5.3 us
  transfers between devices with their start and end apart: 5, of which 3 were waited for; matrix products, arithmetic and copies ran while one was open for 3% of the time, Pallas kernels for 0%

commit v1 on v0

--- a/solution.py
+++ b/solution.py
@@ -1,3 +1,4 @@
+import functools
 import jax
 import jax.numpy as jnp
 from jax import lax
@@ -8,6 +9,13 @@
 CENTRE = 3.0
 RADIUS = 2.0
 RIDGE = 0.01
+
+
+def use_orders(buf, ax_name):
+    return jnp.sum(lax.all_gather(buf, ax_name), axis=0)
+
+
+keep_up_knots_in = functools.partial(use_orders, ax_name="dom")
 
 
 def extended_2(x, sides, width):
@@ -118,7 +126,7 @@
             colsum(-two_im * samples),
         ]
     )
-    second_tot = lax.psum(second_set, "dom")
+    second_tot = keep_up_knots_in(second_set)
     totals = jnp.concatenate([first_tot, second_tot], axis=0)
     g_one = totals[0]
     q_one_re = totals[1]

time: 186 us -> 199 us (1.070)
  blocking collectives: 31.5 us -> 44.6 us
    all_gather x0 -> x1, blocking collectives: none -> 13.4 us  [use_orders(): return jnp.sum(lax.all_gather(buf, ax_name), axis=0)]
where the time goes in v1:
time: 199 us
  waiting for transfers between devices  73.7 us (37%)
  blocking collectives  44.6 us (22%)
  other arithmetic  38.1 us (19%)
  between operations  14.5 us (7%)
  starting transfers between devices  12.2 us (6%)
  local copies, waits for them, and re-layouts  7.97 us (4%)
  matrix products  7.85 us (4%)
    psum x1, waiting for transfers between devices, on_device(): subspace = lax.psum(weighted, 'shift')  60.2 us
    psum x1, blocking collectives, on_device(): reduced_h, reduced_b = lax.psum((part_h, part_b), 'dom')  21.2 us
    sub x2, other arithmetic, shrink_operate(): return combine(inner, onsite_inner * inner - beside)  18.2 us
    all_gather x1, blocking collectives, use_orders(): return jnp.sum(lax.all_gather(buf, ax_name), axis=0)  13.4 us
    psum x1, blocking collectives, on_device(): first_tot = lax.psum(first_set, 'dom')  9.92 us
    ppermute x2, starting transfers between devices, extended_2(): before = lax.ppermute(last, axis, up)  9.55 us
    ppermute x2, waiting for transfers between devices, extended_2(): before = lax.ppermute(last, axis, up)  8.03 us
    ppermute x2, waiting for transfers between devices, extended_2(): after = lax.ppermute(first, axis, down)  5.49 us
  transfers between devices with their start and end apart: 5, of which 3 were waited for; matrix products, arithmetic and copies ran while one was open for 3% of the time, Pallas kernels for 0%

profile of v1, /device:TPU:0, one launch (start us, length us, event | category | flops | bytes accessed | tf_op | source)
XLA Modules:
  0.0 198.9 jit_solution(7608729000263703940)
XLA Ops:
  7.2 1.7 constant_dynamic-update-slice_fusion
  9.7 5.0 %collective-permute-start = (f32[2,65,1024]{2,0,1:T(2,128)S(1)}, f32[2,65,1024]{2,0,1:T(2,128)S(1)}, u32[]{:S(2)}, u32[]{:S(2)}) collective-permute-start(f32[2,65,1024]{2,0,1:T(2,128)S(1)} %copy.8), channel_id=1, source_target_pairs={{0,1},{1,2},{2,3},{4,5},{5,6},{6,7},{8,9},{9,10},{10,11},{12,13},{... | collective-permute-start | bytes 1597448 | tf_op jit(solution)/shard_map/ppermute | solution.py:28
  15.9 1.3 collective-permute-start.1
  18.0 8.0 %collective-permute-done = f32[2,65,1024]{2,0,1:T(2,128)S(1)} collective-permute-done((f32[2,65,1024]{2,0,1:T(2,128)S(1)}, f32[2,65,1024]{2,0,1:T(2,128)S(1)}, u32[]{:S(2)}, u32[]{:S(2)}) %collective-permute-start) | collective-permute-done | bytes 532512 | tf_op jit(solution)/shard_map/ppermute | solution.py:28
  26.1 5.5 %collective-permute-done.1 = f32[2,65,1024]{2,0,1:T(2,128)} collective-permute-done((f32[2,65,1024]{2,0,1:T(2,128)}, f32[2,65,1024]{2,0,1:T(2,128)}, u32[]{:S(2)}, u32[]{:S(2)}) %collective-permute-start.1) | collective-permute-done | bytes 532512 | tf_op jit(solution)/shard_map/ppermute | solution.py:29
  31.6 1.2 copy.11
  34.6 2.8 %fusion.9 = f32[2,10,64,1024]{3,2,1,0:T(8,128)} fusion(f32[1,12,64,1024]{3,2,1,0:T(8,128)S(1)} %get-tuple-element.27, f32[1,12,64,1024]{3,2,1,0:T(8,128)S(1)} %get-tuple-element.26), kind=kLoop, calls=%fused_computation.21 | loop fusion | flops 1310720 | bytes 11534336 | tf_op jit(solution)/shard_map/stack | solution.py:69
  37.4 13.4 %fusion.4 = f32[2,10,64,1024]{3,2,1,0:T(8,128)} fusion(f32[2,10,64,1024]{3,2,1,0:T(8,128)} %fusion.9, f32[1,12,64,1024]{3,2,1,0:T(8,128)S(1)} %get-tuple-element.27, f32[1,12,64,1024]{3,2,1,0:T(8,128)S(1)} %get-tuple-element.26, f32[1024]{0:T(1024)S(1)} %get-tuple-element.43, f32[1024]{0:T(1024)S(1)} %get-tuple-element.42, f32[10,1024]{1,0:T(8,128)S(1)} %bitcast.189), kind=kLoop, calls=%fused_computation.16 | loop fusion | flops 14417920 | bytes 16826368 | tf_op jit(solution)/shard_map/sub | solution.py:90
  50.8 3.8 %slice_subtract_fusion.1 = (f32[1,10,64,1024]{3,2,1,0:T(8,128)S(1)}, f32[1,10,64,1024]{3,2,1,0:T(8,128)S(1)}) fusion(f32[2,10,64,1024]{3,2,1,0:T(8,128)} %fusion.4, f32[1,12,64,1024]{3,2,1,0:T(8,128)S(1)} %get-tuple-element.26, f32[1,12,64,1024]{3,2,1,0:T(8,128)S(1)} %get-tuple-element.27, f32[]{:T(128)S(6)} %mul.491, f32[]{:T(128)S(6)} %add_shard_map.3), kind=kLoop, calls=%fused_computation.43 | loop fusion | flops 5242880 | bytes 15728648 | tf_op jit(solution)/shard_map/sub | solution.py:79
  55.6 1.3 multiply_add_fusion
  57.4 4.8 %fusion.14 = f32[2,8,64,1024]{3,2,1,0:T(8,128)S(1)} fusion(f32[2,8,64,1024]{3,2,1,0:T(8,128)S(1)} %fusion.19, f32[1,10,64,1024]{3,2,1,0:T(8,128)S(1)} %get-tuple-element.25, f32[1,10,64,1024]{3,2,1,0:T(8,128)S(1)} %get-tuple-element.24, f32[1024]{0:T(1024)S(1)} %get-tuple-element.43, f32[1024]{0:T(1024)S(1)} %get-tuple-element.42, f32[8,1024]{1,0:T(8,128)S(1)} %bitcast.190), kind=kLoop, calls=%fused_computation.32 | loop fusion | flops 11534336 | bytes 13672448 | tf_op jit(solution)/shard_map/sub | solution.py:90
  62.3 1.5 fusion.36
  63.9 2.0 %multiply_reduce_fusion.1 = (f32[64]{0:T(128)S(1)}, f32[64]{0:T(128)S(1)}, f32[64]{0:T(128)S(1)}, f32[64]{0:T(128)S(1)}, f32[64]{0:T(128)S(1)}, /*index=5*/f32[64]{0:T(128)S(1)}, f32[64]{0:T(128)S(1)}, f32[64]{0:T(128)S(1)}) fusion(f32[8,64,1024]{2,1,0:T(8,128)S(1)} %copy-done.2, f32[2,10,64,1024]{3,2,1,0:T(8,128)S(1)} %maximum_multiply_fusion, ...), kind=kLoop, calls=%fused_computation.72 | loop fusion | flops 13630976 | bytes 10487808 | tf_op jit(solution)/shard_map/reduce_sum | solution.py:50
  65.9 9.9 %psum.28 = f32[3,64]{1,0:T(4,128)S(1)} all-reduce(f32[3,64]{1,0:T(4,128)S(1)} %pad_maximum_fusion.6), channel_id=1, replica_groups=mesh['shift'=8,'dom'=4] {'dom'}, use_global_device_ids=true, to_apply=%region_9.10 | all-reduce | flops 192 | bytes 1536 | tf_op jit(solution)/shard_map/psum | solution.py:115
  75.9 13.4 %all-gather.1 = f32[4,5,64]{2,1,0:T(8,128)S(1)} all-gather(f32[1,5,64]{2,1,0:T(8,128)S(1)} %bitcast.191), channel_id=2, replica_groups=mesh['shift'=8,'dom'=4] {'dom'}, dimensions={0}, use_global_device_ids=true | all-gather | bytes 6400 | tf_op jit(solution)/shard_map/all_gather | solution.py:15
  89.4 4.9 %multiply_subtract_fusion.1 = f32[8,64,1024]{2,1,0:T(8,128)} fusion(f32[8,64,1024]{2,1,0:T(8,128)S(1)} %copy-done.2, f32[2,10,64,1024]{3,2,1,0:T(8,128)} %copy-done, f32[]{:T(128)S(6)} %div.77, f32[8,1024]{1,0:T(8,128)S(1)} %get-tuple-element.36, f32[64]{0:T(128)S(1)} %fusion.65, f32[8,1024]{1,0:T(8,128)S(1)} %get-tuple-element.37, ...), kind=kLoop, calls=%fused_computation.70 | loop fusion | flops 9961472 | bytes 8455176 | tf_op jit(solution)/shard_map/sub | solution.py:170
  94.3 60.2 %all-reduce.6.cloned.1.call-done = f32[8,64,1024]{2,1,0:T(8,128)} async-done(((f32[8,64,1024]{2,1,0:T(8,128)}), f32[8,64,1024]{2,1,0:T(8,128)}) %all-reduce.6.cloned.1.call-update) | async-done | bytes 2097168 | tf_op jit(solution)/shard_map/psum | solution.py:172
  154.5 1.2 fusion.78
  155.8 1.3 collective-permute-start.2
  157.1 4.6 %collective-permute-start.3 = (f32[1,64,1024]{2,1,0:T(8,128)S(1)}, f32[1,64,1024]{2,1,0:T(8,128)S(1)}, u32[]{:S(2)}, u32[]{:S(2)}) collective-permute-start(f32[1,64,1024]{2,1,0:T(8,128)S(1)} %get-tuple-element.31), channel_id=1, source_target_pairs={{0,1},{1,2},{2,3},{4,5},{5,6},{6,7},{8,9},{9,10},{10,11},{12,13},{... | collective-permute-start | bytes 786440 | tf_op jit(solution)/shard_map/ppermute | solution.py:28
  161.6 4.0 %fusion.41 = f32[64,64]{1,0:T(8,128)S(1)} fusion(f32[8,64,1024]{2,1,0:T(8,128)} %all-reduce.6.cloned.1.call-done), kind=kOutput, calls=%fused_computation.81 | convolution fusion | flops 402657280 | bytes 2113536 | tf_op jit(solution)/shard_map/znc,zmc->nm/dot_general | solution.py:176
  165.7 3.8 %fusion.42 = f32[64,64]{1,0:T(8,128)S(1)} fusion(f32[8,64,1024]{2,1,0:T(8,128)S(1)} %copy-done.1, f32[1,64,1024]{2,1,0:T(8,128)S(1)} %collective-permute-done.3, f32[1,64,1024]{2,1,0:T(8,128)S(1)} %collective-permute-done.2, f32[1024]{0:T(1024)S(1)} %get-tuple-element.43, f32[1024]{0:T(1024)S(1)} %get-tuple-element.42, f32[8,1024]{1,0:T(8,128)S(1)} %copy-done.5), kind=kOutput, calls=%fused_computation.82 | convolution fusion | flops 408424448 | bytes 4775936 | tf_op jit(solution)/shard_map/znc,zmc->nm/dot_general | solution.py:175
  169.5 21.2 %all-reduce.3 = (f32[64,64]{1,0:T(8,128)}, f32[64,64]{1,0:T(8,128)}) all-reduce(f32[64,64]{1,0:T(8,128)S(1)} %fusion.42, f32[64,64]{1,0:T(8,128)S(1)} %fusion.41), channel_id=1, replica_groups=mesh['shift'=8,'dom'=4] {'dom'}, use_global_device_ids=true, to_apply=%region_11.12 | all-reduce | flops 8192 | bytes 65536 | tf_op jit(solution)/shard_map/psum | solution.py:177
  190.8 1.3 copy.40
  (47 shorter events, 6.2 us)
Async XLA Ops:
  7.2 1.8 copy-start.4
  7.2 147.4 %all-reduce.6.cloned.1.call-start = ((), (), s32[]{:S(2)}) async-start(), calls=%async_computation | async-start | bytes 4194304 | tf_op jit(solution)/shard_map/psum | solution.py:172
  9.7 16.3 %collective-permute-start = (f32[2,65,1024]{2,0,1:T(2,128)S(1)}, f32[2,65,1024]{2,0,1:T(2,128)S(1)}, u32[]{:S(2)}, u32[]{:S(2)}) collective-permute-start(f32[2,65,1024]{2,0,1:T(2,128)S(1)} %copy.8), channel_id=1, source_target_pairs={{0,1},{1,2},{2,3},{4,5},{5,6},{6,7},{8,9},{9,10},{10,11},{12,13},{... | collective-permute-start | bytes 1597448 | tf_op jit(solution)/shard_map/ppermute | solution.py:28
  15.9 15.8 %collective-permute-start.1 = (f32[2,65,1024]{2,0,1:T(2,128)}, f32[2,65,1024]{2,0,1:T(2,128)}, u32[]{:S(2)}, u32[]{:S(2)}) collective-permute-start(f32[2,65,1024]{2,0,1:T(2,128)} %copy.9), channel_id=1, source_target_pairs={{1,0},{2,1},{3,2},{5,4},{6,5},{7,6},{9,8},{10,9},{11,10},{13,12},{... | collective-permute-start | bytes 1597448 | tf_op jit(solution)/shard_map/ppermute | solution.py:29
  33.0 0.7 copy-start.3
  50.8 3.9 %slice-start = ((f32[12,1,1024]{2,1,0:T(1,128)}), f32[10,1,1024]{2,1,0:T(1,128)S(1)}, s32[]{:S(2)}) async-start(f32[12,1,1024]{2,1,0:T(1,128)} %copy-done.3), calls=%async_computation.1 | async-start | bytes 81920 | tf_op jit(solution)/shard_map/slice | solution.py:116
  55.6 8.2 %copy-start = (f32[2,10,64,1024]{3,2,1,0:T(8,128)}, f32[2,10,64,1024]{3,2,1,0:T(8,128)S(1)}, u32[]{:S(2)}) copy-start(f32[2,10,64,1024]{3,2,1,0:T(8,128)S(1)} %maximum_multiply_fusion) | copy-start | bytes 15728644
  62.3 1.6 copy-start.2
  94.3 71.4 %copy-start.5 = (f32[8,1024]{1,0:T(8,128)S(1)}, f32[8,1024]{1,0:T(8,128)}, u32[]{:S(2)}) copy-start(f32[8,1024]{1,0:T(8,128)} %get-tuple-element.35) | copy-start | bytes 98308
  154.5 11.2 %copy-start.1 = (f32[8,64,1024]{2,1,0:T(8,128)S(1)}, f32[8,64,1024]{2,1,0:T(8,128)}, u32[]{:S(2)}) copy-start(f32[8,64,1024]{2,1,0:T(8,128)} %all-reduce.6.cloned.1.call-done) | copy-start | bytes 6291460
  155.8 9.9 %collective-permute-start.2 = (f32[1,64,1024]{2,1,0:T(8,128)S(1)}, f32[1,64,1024]{2,1,0:T(8,128)S(1)}, u32[]{:S(2)}, u32[]{:S(2)}) collective-permute-start(f32[1,64,1024]{2,1,0:T(8,128)S(1)} %get-tuple-element.30), channel_id=1, source_target_pairs={{1,0},{2,1},{3,2},{5,4},{6,5},{7,6},{9,8},{10,9},{11,10},{13,12},{... | collective-permute-start | bytes 786440 | tf_op jit(solution)/shard_map/ppermute | solution.py:29
  157.1 8.7 %collective-permute-start.3 = (f32[1,64,1024]{2,1,0:T(8,128)S(1)}, f32[1,64,1024]{2,1,0:T(8,128)S(1)}, u32[]{:S(2)}, u32[]{:S(2)}) collective-permute-start(f32[1,64,1024]{2,1,0:T(8,128)S(1)} %get-tuple-element.31), channel_id=1, source_target_pairs={{0,1},{1,2},{2,3},{4,5},{5,6},{6,7},{8,9},{9,10},{10,11},{12,13},{... | collective-permute-start | bytes 786440 | tf_op jit(solution)/shard_map/ppermute | solution.py:28
Sparse Core Ops, SparseCore 0:
  94.4 60.0 all-reduce.5
